TPU v7x, 64 devices: a 2x2x8 block of a 4x4x8 slice. The times are simulated.
64 devices in a mesh: dp: 4 (over x, y), tp: 16 (over z, core).
Axes of the slice: x: 2, y: 2, z: 8, core: 2. Of those that a mesh axis runs over, the one named last changes fastest.
The devices are a block of a 4x4x8 slice.
Arguments:
- y_one: float32 [192, 64, 1024], P('dp'), parts along dimension 0
- y_two: float32 [192, 64, 1024], P('dp'), parts along dimension 0
- dy_one: float32 [192, 64, 1024], P('dp'), parts along dimension 0
- dy_two: float32 [192, 64, 1024], P('dp'), parts along dimension 0
- seq_lens: int32 [192], P('dp'), parts along dimension 0
- w_query: bfloat16 [1, 1024, 16, 128], P(None, None, 'tp')
- w_key: bfloat16 [1, 1024, 16, 128], P(None, None, 'tp')
- w_value: bfloat16 [1, 1024, 16, 128], P(None, None, 'tp')
- w_out: bfloat16 [1, 16, 128, 1024], P(None, 'tp')
- w_up: bfloat16 [1, 1024, 3072], P(None, None, 'tp')
- w_down: bfloat16 [1, 3072, 1024], P(None, 'tp')
Outputs:
- output 1: float32 [192, 64, 1024], P('dp'), parts along dimension 0
- output 2: float32 [192, 64, 1024], P('dp'), parts along dimension 0
- output 3: float32 [192, 64, 1024], P('dp'), parts along dimension 0
- output 4: float32 [192, 64, 1024], P('dp'), parts along dimension 0
- output 5: float32 [4, 1024, 16, 128], P('dp', None, 'tp'), parts along dimension 0
- output 6: float32 [4, 1024, 16, 128], P('dp', None, 'tp'), parts along dimension 0
- output 7: float32 [4, 1024, 16, 128], P('dp', None, 'tp'), parts along dimension 0
- output 8: float32 [4, 16, 128, 1024], P('dp', 'tp'), parts along dimension 0
- output 9: float32 [4, 1024, 3072], P('dp', None, 'tp'), parts along dimension 0
- output 10: float32 [4, 3072, 1024], P('dp', 'tp'), parts along dimension 0
There are 4 independent parts. A program takes and returns all parts, laid end to end along the dimension named above; an argument that names none is the same for every part.
All inputs are finite; a program needn't handle non-finite values.
Results may differ from a plain program's by a relative error of at most 0.0067854.
Values are sent between devices in bfloat16 or wider.
A program may use at most 768 MiB of HBM per device.

v0:
```python
import jax
import jax.numpy as jnp
from jax import lax
from jax.sharding import PartitionSpec as P, NamedSharding

F32 = jnp.float32
BF16 = jnp.bfloat16
EPS = 1e-5
MASK_VALUE = -1e30


def rms_norm(x_val):
    inv_rms = lax.rsqrt(jnp.mean(x_val * x_val, axis=-1, keepdims=True) + EPS)
    return x_val * inv_rms, inv_rms


def rms_back(normed, inv_rms, grad_norm):
    return inv_rms * (grad_norm - normed * jnp.mean(grad_norm * normed, axis=-1, keepdims=True))


def visible_mask(seq_lens, seq_len):
    row_pos = lax.broadcasted_iota(jnp.int32, (seq_len, seq_len), 0)
    col_pos = lax.broadcasted_iota(jnp.int32, (seq_len, seq_len), 1)
    causal = (col_pos <= row_pos)[None, None, None]
    in_length = col_pos[None, None, None] < seq_lens[:, None, None, None, None]
    return causal & in_length


def block_back(carry, seq_lens, layer_w, all_reduce):
    y_one, y_two, dy_one, dy_two = carry
    w_query, w_key, w_value, w_out, w_up, w_down = layer_w
    n_batch, seq_len = y_one.shape[0], y_one.shape[1]
    n_heads, head_dim = w_query.shape[1], w_query.shape[2]
    kv_slots = w_key.shape[1]
    group_size = n_heads // kv_slots
    score_scale = head_dim ** -0.5

    norm_g, inv_g = rms_norm(y_one)
    norm_g_b = norm_g.astype(BF16)
    pre_act = jnp.einsum('bsd,df->bsf', norm_g_b, w_up, preferred_element_type=F32)
    act_val, gelu_back = jax.vjp(jax.nn.gelu, pre_act)
    act_b = act_val.astype(BF16)
    x_two = y_two - all_reduce(jnp.einsum('bsf,fd->bsd', act_b, w_down, preferred_element_type=F32))
    dy2_b = dy_two.astype(BF16)
    d_act = jnp.einsum('bsd,fd->bsf', dy2_b, w_down, preferred_element_type=F32)
    d_pre = gelu_back(d_act)[0].astype(BF16)
    dw_down = jnp.einsum('bsf,bsd->fd', act_b, dy2_b, preferred_element_type=F32)
    dw_up = jnp.einsum('bsd,bsf->df', norm_g_b, d_pre, preferred_element_type=F32)
    grad_norm_g = all_reduce(jnp.einsum('bsf,df->bsd', d_pre, w_up, preferred_element_type=F32))
    dy_one = dy_one + rms_back(norm_g, inv_g, grad_norm_g)

    norm_f, inv_f = rms_norm(x_two)
    norm_f_b = norm_f.astype(BF16)
    query_proj = jnp.einsum('bsd,dhe->bshe', norm_f_b, w_query, preferred_element_type=F32).astype(BF16)
    query_grp = query_proj.reshape(n_batch, seq_len, kv_slots, group_size, head_dim)
    key_proj = jnp.einsum('bsd,dge->bsge', norm_f_b, w_key, preferred_element_type=F32).astype(BF16)
    value_proj = jnp.einsum('bsd,dge->bsge', norm_f_b, w_value, preferred_element_type=F32).astype(BF16)
    scores = jnp.einsum('bigre,bjge->bgrij', query_grp, key_proj, preferred_element_type=F32) * score_scale
    scores = jnp.where(visible_mask(seq_lens, seq_len), scores, MASK_VALUE)
    attn_probs = jax.nn.softmax(scores, axis=-1)
    probs_b = attn_probs.astype(BF16)
    attn_out = jnp.einsum('bgrij,bjge->bigre', probs_b, value_proj, preferred_element_type=F32).astype(BF16)
    attn_out = attn_out.reshape(n_batch, seq_len, n_heads, head_dim)
    x_one = y_one - all_reduce(jnp.einsum('bihe,hed->bid', attn_out, w_out, preferred_element_type=F32))
    dy1_b = dy_one.astype(BF16)
    dw_out = jnp.einsum('bihe,bid->hed', attn_out, dy1_b, preferred_element_type=F32)
    d_attn = jnp.einsum('bid,hed->bihe', dy1_b, w_out, preferred_element_type=F32).astype(BF16)
    d_attn = d_attn.reshape(n_batch, seq_len, kv_slots, group_size, head_dim)
    d_value = jnp.einsum('bgrij,bigre->bjge', probs_b, d_attn, preferred_element_type=F32).astype(BF16)
    d_probs = jnp.einsum('bigre,bjge->bgrij', d_attn, value_proj, preferred_element_type=F32)
    d_scores = (attn_probs * (d_probs - jnp.sum(d_probs * attn_probs, axis=-1, keepdims=True)) * score_scale).astype(BF16)
    d_query = jnp.einsum('bgrij,bjge->bigre', d_scores, key_proj, preferred_element_type=F32).astype(BF16)
    d_query = d_query.reshape(n_batch, seq_len, n_heads, head_dim)
    d_key = jnp.einsum('bgrij,bigre->bjge', d_scores, query_grp, preferred_element_type=F32).astype(BF16)
    dw_query = jnp.einsum('bsd,bshe->dhe', norm_f_b, d_query, preferred_element_type=F32)
    dw_key = jnp.einsum('bsd,bsge->dge', norm_f_b, d_key, preferred_element_type=F32)
    dw_value = jnp.einsum('bsd,bsge->dge', norm_f_b, d_value, preferred_element_type=F32)
    grad_norm_f = all_reduce(jnp.einsum('bshe,dhe->bsd', d_query, w_query, preferred_element_type=F32)
                             + jnp.einsum('bsge,dge->bsd', d_key, w_key, preferred_element_type=F32)
                             + jnp.einsum('bsge,dge->bsd', d_value, w_value, preferred_element_type=F32))
    dx_two = dy_two + rms_back(norm_f, inv_f, grad_norm_f)
    return (x_one, x_two, dy_one, dx_two), (dw_query, dw_key, dw_value, dw_out, dw_up, dw_down)


def stack_grads(grads_by_layer):
    return tuple(jnp.stack([layer_grads[grad_pos] for layer_grads in grads_by_layer]) for grad_pos in range(6))


def tp_sum(partial_val):
    return lax.psum(partial_val, 'tp')


def solution(mesh):
    act_spec = P('dp', None, None)
    w_specs = (P(None, None, 'tp', None), P(None, None, 'tp', None), P(None, None, 'tp', None),
               P(None, 'tp', None, None), P(None, None, 'tp'), P(None, 'tp', None))
    g_specs = (P('dp', None, 'tp', None), P('dp', None, 'tp', None), P('dp', None, 'tp', None),
               P('dp', 'tp', None, None), P('dp', None, 'tp'), P('dp', 'tp', None))

    def local_fn(y_one, y_two, dy_one, dy_two, seq_lens, w_query, w_key, w_value, w_out, w_up, w_down):
        weights = (w_query, w_key, w_value, w_out, w_up, w_down)
        carry = (y_one, y_two, dy_one, dy_two)
        n_layers = w_query.shape[0]
        grads_by_layer = [None] * n_layers
        for layer_idx in reversed(range(n_layers)):
            layer_w = tuple(w_stack[layer_idx] for w_stack in weights)
            carry, grads_by_layer[layer_idx] = block_back(carry, seq_lens, layer_w, tp_sum)
        return carry + stack_grads(grads_by_layer)

    return jax.shard_map(local_fn, mesh=mesh,
                         in_specs=(act_spec,) * 4 + (P('dp'),) + w_specs,
                         out_specs=(act_spec,) * 4 + g_specs,
                         check_vma=False)
```

profile of v0, /device:TPU:21, one launch (start us, length us, event | category | flops | bytes accessed | tf_op | source)
XLA Modules:
  0.0 731.2 jit_solution(795516830341834828)
XLA Ops:
  7.2 0.0 copy-start
  7.2 0.1 all-reduce.7.cloned.1.call-start
  7.3 5.6 multiply_reduce_fusion.3
  12.9 2.6 copy-done.2
  15.5 3.1 fusion.16
  18.6 0.0 slice-start.8
  18.6 6.8 fusion.44
  25.4 0.0 copy-start.12
  25.4 3.6 fusion.6
  29.0 1.2 copy-done.5
  30.2 6.6 fusion.46
  36.8 0.1 all-reduce.7.cloned.1.call-update
  36.8 0.2 all-reduce.5.cloned.1.call-start
  37.1 281.6 %all-reduce.7.cloned.1.call-done = (f32[48,64,1024]{2,1,0:T(8,128)}, f32[48,64,1024]{2,1,0:T(8,128)}) async-done(((f32[48,64,1024]{2,1,0:T(8,128)}, f32[48,64,1024]{2,1,0:T(8,128)}), (f32[48,64,1024]{2,1,0:T(8,128)}, f32[48,64,1024]{2,1,0:T(8,128)})) %all-reduce.7.cloned.1.call-update) | async-done | bytes 25165840 | tf_op jit(solution)/shard_map/psum | solution.py:90
  318.7 21.4 %multiply_reduce_fusion.2 = (f32[48,64]{1,0:T(8,128)S(1)}, f32[48,64,1024]{2,1,0:T(8,128)}, f32[48,64]{1,0:T(8,128)S(1)}) fusion(f32[48,64,1024]{2,1,0:T(8,128)} %param.12, f32[48,64,1024]{2,1,0:T(8,128)} %get-tuple-element.22, f32[48,64,1024]{2,1,0:T(8,128)} %get-tuple-element.23, f32[48,64,1024]{2,1,0:T(8,128)} %param.11, f32[48,64]{1,0:T(8,128)S(1)} %copy-done.15), kind=kLoop, calls=%fused_computation.5 | loop fusion | flops 18868224 | bytes 62951424 | tf_op jit(solution)/shard_map/reduce_sum | solution.py:13
  340.1 8.1 %multiply_convert_fusion = bf16[48,64,1024]{2,1,0:T(8,128)(2,1)} fusion(f32[48,64,1024]{2,1,0:T(8,128)} %get-tuple-element.25, f32[48,64]{1,0:T(8,128)S(1)} %add_rsqrt_fusion), kind=kLoop, calls=%fused_computation.7 | loop fusion | flops 6291456 | bytes 18886656 | tf_op jit(solution)/shard_map/convert_element_type | solution.py:53
  348.2 4.7 convolution_convert_fusion.4
  353.0 1.9 convolution_convert_fusion.5
  354.9 1.9 convolution_convert_fusion.6
  356.8 13.4 %multiply_add_fusion.1 = f32[48,64,1024]{2,1,0:T(8,128)S(1)} fusion(f32[48,64,1024]{2,1,0:T(8,128)} %param.13, f32[48,64,1024]{2,1,0:T(8,128)} %get-tuple-element.23, f32[48,64,1024]{2,1,0:T(8,128)} %param.11, f32[48,64]{1,0:T(8,128)S(1)} %broadcast_multiply_fusion.1, f32[48,64]{1,0:T(8,128)S(1)} %copy-done.15), kind=kLoop, calls=%fused_computation.3 | loop fusion | flops 15728640 | bytes 50356224 | tf_op jit(solution)/shard_map/add | solution.py:50
  370.2 1.9 fusion.24
  372.1 2.9 copy-done.3
  374.9 0.6 fusion.64
  375.6 0.4 fusion.28
  375.9 1.3 fusion.32
  377.2 0.5 fusion.29
  377.7 2.0 fusion.19
  379.7 0.6 fusion.40
  380.3 0.4 fusion.31
  380.7 0.4 fusion.30
  381.2 6.6 fusion.60
  387.7 1.8 fusion.53
  389.6 6.6 fusion.56
  396.2 11.7 %add_add_fusion = f32[48,64,1024]{2,1,0:T(8,128)} fusion(f32[48,64,1024]{2,1,0:T(8,128)} %fusion.56, f32[48,64,1024]{2,1,0:T(8,128)S(1)} %fusion.53, bf16[48,64,128]{2,1,0:T(8,128)(2,1)S(1)} %copy-done.16, bf16[1,1024,1,128]{3,1,2,0:T(8,128)(2,1)S(1)} %copy-done.20), kind=kOutput, calls=%fused_computation.2 | convolution fusion | flops 811597824 | bytes 38797312 | tf_op jit(solution)/shard_map/bsge,dge->bsd/dot_general | solution.py:80
  407.8 0.1 all-reduce.5.cloned.1.call-update
  407.9 7.6 %fusion.33 = f32[1,1024,192]{1,2,0:T(8,128)} fusion(bf16[48,64,192]{2,1,0:T(8,128)(2,1)} %copy-done.5, f32[48,64,1024]{2,1,0:T(8,128)} %param.11, f32[48,64]{1,0:T(8,128)S(1)} %copy-done.15), kind=kOutput, calls=%fused_computation.53 | convolution fusion | flops 1214251008 | bytes 14561280 | tf_op jit(solution)/shard_map/bsd,bsf->df/dot_general | solution.py:48
  415.6 7.5 %fusion.34 = f32[1,192,1024]{2,1,0:T(8,128)} fusion(f32[48,64,1024]{2,1,0:T(8,128)} %param.14, f32[48,64,192]{2,1,0:T(8,128)S(1)} %fusion.16), kind=kOutput, calls=%fused_computation.54 | convolution fusion | flops 1216413696 | bytes 15728640 | tf_op jit(solution)/shard_map/bsf,bsd->fd/dot_general | solution.py:47
  423.1 2.6 fusion.67
  425.7 2.6 fusion.65
  428.3 2.6 fusion.66
  430.9 0.0 slice-done.5
  431.0 0.1 copy-done.11
  431.1 1.8 fusion.37
  432.9 251.4 %all-reduce.5.cloned.1.call-done = (f32[48,64,1024]{2,1,0:T(8,128)}, f32[48,64,1024]{2,1,0:T(8,128)}) async-done(((f32[48,64,1024]{2,1,0:T(8,128)}, f32[48,64,1024]{2,1,0:T(8,128)}), (f32[48,64,1024]{2,1,0:T(8,128)}, f32[48,64,1024]{2,1,0:T(8,128)})) %all-reduce.5.cloned.1.call-update) | async-done | bytes 25165840 | tf_op jit(solution)/shard_map/psum | solution.py:90
  684.3 15.9 %sub.34 = f32[48,64,1024]{2,1,0:T(8,128)} subtract(f32[48,64,1024]{2,1,0:T(8,128)} %param.11, f32[48,64,1024]{2,1,0:T(8,128)} %get-tuple-element.20) | non-fusion elementwise | flops 3145728 | bytes 37748736 | tf_op jit(solution)/shard_map/sub | solution.py:64
  700.2 9.2 %multiply_reduce_fusion = f32[48,64]{1,0:T(8,128)S(1)} fusion(f32[48,64,1024]{2,1,0:T(8,128)} %get-tuple-element.21, f32[48,64,1024]{2,1,0:T(8,128)} %get-tuple-element.25, f32[48,64]{1,0:T(8,128)S(1)} %add_rsqrt_fusion), kind=kLoop, calls=%fused_computation.1 | loop fusion | flops 9434112 | bytes 25190400 | tf_op jit(solution)/shard_map/reduce_sum | solution.py:18
  709.4 0.2 slice-done.2
  709.6 14.3 %multiply_add_fusion = f32[48,64,1024]{2,1,0:T(8,128)} fusion(f32[48,64,1024]{2,1,0:T(8,128)} %param.14, f32[48,64,1024]{2,1,0:T(8,128)} %get-tuple-element.21, f32[48,64,1024]{2,1,0:T(8,128)S(1)} %bitcast.142, f32[48,64]{1,0:T(8,128)S(1)} %broadcast_multiply_fusion, f32[48,64]{1,0:T(8,128)} %copy-done.18), kind=kLoop, calls=%fused_computation | loop fusion | flops 15728640 | bytes 50356224 | tf_op jit(solution)/shard_map/add | solution.py:81
  (76 shorter events, 0.2 us)
Async XLA Ops:
  7.2 11.4 %copy-start = (bf16[1,192,1024]{2,1,0:T(8,128)(2,1)S(1)}, bf16[1,192,1024]{2,1,0:T(8,128)(2,1)}, u32[]{:S(2)}) copy-start(bf16[1,192,1024]{2,1,0:T(8,128)(2,1)} %param.21) | copy-start | bytes 1179652
  7.2 311.5 %all-reduce.7.cloned.1.call-start = ((), (), s32[]{:S(2)}) async-start(), calls=%async_computation.1 | async-start | bytes 50331648 | tf_op jit(solution)/shard_map/psum | solution.py:90
  7.3 8.2 %copy-start.2 = (f32[48,64,1024]{2,1,0:T(8,128)S(1)}, f32[48,64,1024]{2,1,0:T(8,128)}, u32[]{:S(2)}) copy-start(f32[48,64,1024]{2,1,0:T(8,128)} %param.11) | copy-start | bytes 37748740
  15.5 3.1 copy-start.14
  15.5 10.0 %slice-start.6 = ((s8[12582912]{0:T(1024)(128)(4,1)}), s8[4194304]{0:T(1024)(128)(4,1)S(1)}, s32[]{:S(2)}) async-start(s8[12582912]{0:T(1024)(128)(4,1)} %bitcast.145), calls=%async_computation.8 | async-start | bytes 8388608
  15.5 10.0 %slice-start.7 = ((s8[12582912]{0:T(1024)(128)(4,1)}), s8[4194304]{0:T(1024)(128)(4,1)S(1)}, s32[]{:S(2)}) async-start(s8[12582912]{0:T(1024)(128)(4,1)} %bitcast.145), calls=%async_computation.9 | async-start | bytes 8388608
  18.6 6.8 slice-start.8
  25.4 4.7 copy-start.12
  29.0 1.2 copy-start.5
  36.8 281.9 %copy-start.15 = (f32[48,64]{1,0:T(8,128)S(1)}, f32[48,64]{1,0:T(8,128)}, u32[]{:S(2)}) copy-start(f32[48,64]{1,0:T(8,128)} %copy-done.14) | copy-start | bytes 36868
  36.8 647.5 %all-reduce.5.cloned.1.call-start = ((), (), s32[]{:S(2)}) async-start(), calls=%async_computation | async-start | bytes 50331648 | tf_op jit(solution)/shard_map/psum | solution.py:90
  340.1 360.1 %copy-start.18 = (f32[48,64]{1,0:T(8,128)}, f32[48,64]{1,0:T(8,128)S(1)}, u32[]{:S(2)}) copy-start(f32[48,64]{1,0:T(8,128)S(1)} %add_rsqrt_fusion) | copy-start | bytes 36868
  340.1 8.1 %copy-start.23 = (bf16[1,1024,1,128]{3,1,2,0:T(8,128)(2,1)S(1)}, bf16[1,1024,1,128]{3,1,2,0:T(8,128)(2,1)}, u32[]{:S(2)}) copy-start(bf16[1,1024,1,128]{3,1,2,0:T(8,128)(2,1)} %param.16) | copy-start | bytes 786436
  348.2 4.7 copy-start.4
  348.2 4.7 copy-start.21
  353.0 1.9 copy-start.19
  356.7 20.5 %copy-start.26 = (bf16[48,64,128]{2,1,0:T(8,128)(2,1)}, bf16[48,64,128]{2,1,0:T(8,128)(2,1)S(1)}, u32[]{:S(2)}) copy-start(bf16[48,64,128]{2,1,0:T(8,128)(2,1)S(1)} %convolution_convert_fusion.6) | copy-start | bytes 2359300
  356.7 13.4 %copy-start.13 = (bf16[1,1,128,1024]{3,2,1,0:T(8,128)(2,1)S(1)}, bf16[1,1,128,1024]{3,2,1,0:T(8,128)(2,1)}, u32[]{:S(2)}) copy-start(bf16[1,1,128,1024]{3,2,1,0:T(8,128)(2,1)} %param.19) | copy-start | bytes 786436
  370.2 4.8 copy-start.3
  370.2 4.8 copy-start.25
  377.7 3.4 copy-start.10
  380.7 7.0 copy-start.6
  381.2 8.4 %copy-start.8 = (bf16[48,64,128]{2,1,0:T(8,128)(2,1)}, bf16[48,64,128]{2,1,0:T(8,128)(2,1)S(1)}, u32[]{:S(2)}) copy-start(bf16[48,64,128]{2,1,0:T(8,128)(2,1)S(1)} %fusion.30) | copy-start | bytes 2359300
  381.2 6.6 copy-start.22
  387.7 1.8 copy-start.24
  389.6 6.6 copy-start.16
  389.6 6.6 copy-start.20
  407.9 15.1 %slice-start.9 = ((s8[6291456]{0:T(1024)(128)(4,1)}), s8[4194304]{0:T(1024)(128)(4,1)S(1)}, s32[]{:S(2)}) async-start(s8[6291456]{0:T(1024)(128)(4,1)} %bitcast.147), calls=%async_computation.11 | async-start | bytes 8388608
  415.6 7.5 %slice-start.10 = ((s8[6291456]{0:T(1024)(128)(4,1)}), s8[2097152]{0:T(1024)(128)(4,1)S(1)}, s32[]{:S(2)}) async-start(s8[6291456]{0:T(1024)(128)(4,1)} %bitcast.147), calls=%async_computation.12 | async-start | bytes 4194304
  415.6 7.5 %copy-start.17 = (bf16[48,64,128]{2,1,0:T(8,128)(2,1)S(1)}, bf16[48,64,128]{2,1,0:T(8,128)(2,1)}, u32[]{:S(2)}) copy-start(bf16[48,64,128]{2,1,0:T(8,128)(2,1)} %fusion.32) | copy-start | bytes 2359300
  423.0 2.6 copy-start.9
  425.7 2.6 copy-start.7
  425.7 5.3 slice-start.3
  425.7 5.3 slice-start.4
  428.3 2.7 slice-start.5
  428.3 2.8 copy-start.11
  684.3 25.1 %slice-start = ((s8[12582912]{0:T(1024)(128)(4,1)}), s8[4194304]{0:T(1024)(128)(4,1)S(1)}, s32[]{:S(2)}) async-start(s8[12582912]{0:T(1024)(128)(4,1)} %bitcast.141), calls=%async_computation.2 | async-start | bytes 8388608
  684.3 25.1 %slice-start.1 = ((s8[12582912]{0:T(1024)(128)(4,1)}), s8[4194304]{0:T(1024)(128)(4,1)S(1)}, s32[]{:S(2)}) async-start(s8[12582912]{0:T(1024)(128)(4,1)} %bitcast.141), calls=%async_computation.3 | async-start | bytes 8388608
  700.2 9.4 %slice-start.2 = ((s8[12582912]{0:T(1024)(128)(4,1)}), s8[4194304]{0:T(1024)(128)(4,1)S(1)}, s32[]{:S(2)}) async-start(s8[12582912]{0:T(1024)(128)(4,1)} %bitcast.141), calls=%async_computation.4 | async-start | bytes 8388608
  709.6 14.3 %copy-start.1 = (bf16[1,192,1024]{2,1,0:T(8,128)(2,1)S(1)}, bf16[1,192,1024]{2,1,0:T(8,128)(2,1)}, u32[]{:S(2)}) copy-start(bf16[1,192,1024]{2,1,0:T(8,128)(2,1)} %param.21) | copy-start | bytes 1179652
Sparse Core Ops, SparseCore 0:
  36.9 281.6 all-reduce.6
  408.0 276.2 all-reduce.4
where the time goes:
time: 738 us; the launch traced here: 731 us
  waiting for transfers between devices  533 us (72%)
  other arithmetic  88.9 us (12%)
  matrix products  86.9 us (12%)
  between operations  14.9 us (2%)
    psum x2, waiting for transfers between devices, tp_sum(): return lax.psum(partial_val, 'tp')  533 us
    reduce_sum x2, other arithmetic, rms_norm(): inv_rms = lax.rsqrt(jnp.mean(x_val * x_val, axis=-1, keepdims=True) + EPS)  27 us
    sub x1, other arithmetic, block_back(): y_one - all_reduce(jnp.einsum('bihe,hed->bid', attn_out, w_out, preferred...  15.9 us
  transfers between devices with their start and end apart: 2, of which 2 were waited for; matrix products, arithmetic and copies ran while one was open for 3% of the time, Pallas kernels for 0%

commit v1 on v0

v1 whole, which is shorter than its diff:
```python
import jax
import jax.numpy as jnp
from jax import lax
from jax.sharding import PartitionSpec as P

F32 = jnp.float32
BF16 = jnp.bfloat16
EPS = 1e-5
MASK_VALUE = -1e30


def rms_norm(x_val):
    inv_rms = lax.rsqrt(jnp.mean(x_val * x_val, axis=-1, keepdims=True) + EPS)
    return x_val * inv_rms, inv_rms


def rms_back(normed, inv_rms, grad_norm):
    return inv_rms * (grad_norm - normed * jnp.mean(grad_norm * normed, axis=-1, keepdims=True))


def visible_mask(seq_lens, seq_len):
    row_pos = lax.broadcasted_iota(jnp.int32, (seq_len, seq_len), 0)
    col_pos = lax.broadcasted_iota(jnp.int32, (seq_len, seq_len), 1)
    causal = (col_pos <= row_pos)[None, None]
    in_length = col_pos[None, None] < seq_lens[:, None, None, None]
    return causal & in_length


def dot(spec, a, b):
    return jnp.einsum(spec, a, b, preferred_element_type=F32)


def block_back(carry, seq_lens, layer_w, tp_idx):
    y_one, y_two, dy_one, dy_two = carry
    own_q, own_k, own_v, own_o, own_up, own_down = layer_w
    seq_len = y_one.shape[1]
    head_dim = own_q.shape[2]
    score_scale = head_dim ** -0.5

    def gathered(w, axis):
        full = lax.all_gather(w, 'tp', axis=axis, tiled=True)
        size = w.shape[axis]
        return jnp.roll(full, -tp_idx * size, axis=axis)

    w_up, w_down = gathered(own_up, 1), gathered(own_down, 0)
    w_query, w_key, w_value, w_out = gathered(own_q, 1), gathered(own_k, 1), gathered(own_v, 1), gathered(own_o, 0)
    own_ff = own_up.shape[1]

    norm_g, inv_g = rms_norm(y_one)
    norm_g_b = norm_g.astype(BF16)
    pre_act = dot('bsd,df->bsf', norm_g_b, w_up)
    act_val, gelu_back = jax.vjp(jax.nn.gelu, pre_act)
    act_b = act_val.astype(BF16)
    x_two = y_two - dot('bsf,fd->bsd', act_b, w_down)
    dy2_b = dy_two.astype(BF16)
    d_act = dot('bsd,fd->bsf', dy2_b, w_down)
    d_pre = gelu_back(d_act)[0].astype(BF16)
    dw_down = dot('bsf,bsd->fd', act_b[..., :own_ff], dy2_b)
    dw_up = dot('bsd,bsf->df', norm_g_b, d_pre[..., :own_ff])
    grad_norm_g = dot('bsf,df->bsd', d_pre, w_up)
    dy_one = dy_one + rms_back(norm_g, inv_g, grad_norm_g)

    norm_f, inv_f = rms_norm(x_two)
    norm_f_b = norm_f.astype(BF16)
    query = dot('bsd,dhe->bshe', norm_f_b, w_query).astype(BF16)
    key = dot('bsd,dhe->bshe', norm_f_b, w_key).astype(BF16)
    value = dot('bsd,dhe->bshe', norm_f_b, w_value).astype(BF16)
    scores = dot('bihe,bjhe->bhij', query, key) * score_scale
    scores = jnp.where(visible_mask(seq_lens, seq_len), scores, MASK_VALUE)
    probs = jax.nn.softmax(scores, axis=-1)
    probs_b = probs.astype(BF16)
    attn = dot('bhij,bjhe->bihe', probs_b, value).astype(BF16)
    x_one = y_one - dot('bihe,hed->bid', attn, w_out)
    dy1_b = dy_one.astype(BF16)
    dw_out = dot('bihe,bid->hed', attn[:, :, :1], dy1_b)
    d_attn = dot('bid,hed->bihe', dy1_b, w_out).astype(BF16)
    d_value = dot('bhij,bihe->bjhe', probs_b, d_attn).astype(BF16)
    d_probs = dot('bihe,bjhe->bhij', d_attn, value)
    d_scores = (probs * (d_probs - jnp.sum(d_probs * probs, axis=-1, keepdims=True)) * score_scale).astype(BF16)
    d_query = dot('bhij,bjhe->bihe', d_scores, key).astype(BF16)
    d_key = dot('bhij,bihe->bjhe', d_scores, query).astype(BF16)
    dw_query = dot('bsd,bshe->dhe', norm_f_b, d_query[:, :, :1])
    dw_key = dot('bsd,bshe->dhe', norm_f_b, d_key[:, :, :1])
    dw_value = dot('bsd,bshe->dhe', norm_f_b, d_value[:, :, :1])
    grad_norm_f = (dot('bshe,dhe->bsd', d_query, w_query) + dot('bshe,dhe->bsd', d_key, w_key)
                   + dot('bshe,dhe->bsd', d_value, w_value))
    dx_two = dy_two + rms_back(norm_f, inv_f, grad_norm_f)
    return (x_one, x_two, dy_one, dx_two), (dw_query, dw_key, dw_value, dw_out, dw_up, dw_down)


def stack_grads(grads_by_layer):
    return tuple(jnp.stack([layer_grads[grad_pos] for layer_grads in grads_by_layer]) for grad_pos in range(6))


def solution(mesh):
    act_spec = P('dp', None, None)
    w_specs = (P(None, None, 'tp', None), P(None, None, 'tp', None), P(None, None, 'tp', None),
               P(None, 'tp', None, None), P(None, None, 'tp'), P(None, 'tp', None))
    g_specs = (P('dp', None, 'tp', None), P('dp', None, 'tp', None), P('dp', None, 'tp', None),
               P('dp', 'tp', None, None), P('dp', None, 'tp'), P('dp', 'tp', None))

    def local_fn(y_one, y_two, dy_one, dy_two, seq_lens, w_query, w_key, w_value, w_out, w_up, w_down):
        weights = (w_query, w_key, w_value, w_out, w_up, w_down)
        carry = (y_one, y_two, dy_one, dy_two)
        n_layers = w_query.shape[0]
        tp_idx = lax.axis_index('tp')
        grads_by_layer = [None] * n_layers
        for layer_idx in reversed(range(n_layers)):
            layer_w = tuple(w_stack[layer_idx] for w_stack in weights)
            carry, grads_by_layer[layer_idx] = block_back(carry, seq_lens, layer_w, tp_idx)
        return carry + stack_grads(grads_by_layer)

    return jax.shard_map(local_fn, mesh=mesh,
                         in_specs=(act_spec,) * 4 + (P('dp'),) + w_specs,
                         out_specs=(act_spec,) * 4 + g_specs,
                         check_vma=False)
```

time: 738 us -> 638 us (0.86)
  waiting for transfers between devices: 533 us -> 43.3 us
  matrix products: 86.9 us -> 512 us
  other arithmetic: 88.9 us -> 50 us
    psum x2 -> x0, waiting for transfers between devices: 533 us -> none  [tp_sum(): return lax.psum(partial_val, 'tp')]
    dot_general x24 -> x23, matrix products: 86.9 us -> 490 us  [dot(): return jnp.einsum(spec, a, b, preferred_element_type=F32)]
    all_gather x0 -> x6, waiting for transfers between devices: none -> 39.5 us  [gathered(): full = lax.all_gather(w, 'tp', axis=axis, tiled=True)]
    sub x0 -> x1, matrix products: none -> 22.3 us  [block_back(): probs = jax.nn.softmax(scores, axis=-1)]
    reduce_sum x2 -> x1, other arithmetic: 27 us -> 5.46 us  [rms_norm(): inv_rms = lax.rsqrt(jnp.mean(x_val * x_val, axis=-1, keepdims=True) + EPS)]
    sub x1 -> x0, other arithmetic: 15.9 us -> none  [block_back(): y_one - all_reduce(jnp.einsum('bihe,hed->bid', attn_out, w_out, preferred...]
    reduce_sum x2 -> x0, other arithmetic: 9.53 us -> none  [the longest x1 9.18 us: rms_back(): jnp.mean(grad_norm * normed, axis=-1, keepdims=True)]
    all_gather x0 -> x1, local copies, waits for them, and re-layouts: none -> 8.61 us  [gathered(): full = lax.all_gather(w, 'tp', axis=axis, tiled=True)]
  transfers between devices with their start and end apart: 2 -> 6, of which waited for: 2 -> 1; matrix products, arithmetic and copies ran while one was open for 3% -> 43% of each run, Pallas kernels for 0% -> 0%
where the time goes in v1:
time: 638 us; the launch traced here: 630 us
  matrix products  512 us (80%)
  other arithmetic  50 us (8%)
  waiting for transfers between devices  43.3 us (7%)
  between operations  14.5 us (2%)
  local copies, waits for them, and re-layouts  9.24 us (1%)
    dot_general x23, matrix products, dot(): return jnp.einsum(spec, a, b, preferred_element_type=F32)  490 us
    all_gather x6, waiting for transfers between devices, gathered(): full = lax.all_gather(w, 'tp', axis=axis, tiled=True)  39.5 us
    sub x1, matrix products, block_back(): probs = jax.nn.softmax(scores, axis=-1)  22.3 us
    add x1, other arithmetic, block_back(): dx_two = dy_two + rms_back(norm_f, inv_f, grad_norm_f)  17.7 us
    add x1, other arithmetic, block_back(): dy_one = dy_one + rms_back(norm_g, inv_g, grad_norm_g)  17.7 us
  transfers between devices with their start and end apart: 6, of which 1 were waited for; matrix products, arithmetic and copies ran while one was open for 43% of the time, Pallas kernels for 0%

profile of v1, /device:TPU:21, one launch (start us, length us, event | category | flops | bytes accessed | tf_op | source)
XLA Modules:
  0.0 629.6 jit_solution(10208539999442273498)
XLA Ops:
  7.2 0.1 all-gather.13.cloned.1.call-start
  7.3 0.7 all-gather.13.cloned.1.call-update
  8.0 0.1 all-gather.15.cloned.1.call-start
  8.1 0.7 all-gather.15.cloned.1.call-update
  8.8 0.1 all-gather.19.cloned.1.call-start
  8.9 0.7 all-gather.19.cloned.1.call-update
  9.6 0.1 all-gather.21.cloned.1.call-start
  9.7 0.6 all-gather.21.cloned.1.call-update
  10.2 0.1 all-gather.17.cloned.1.call-start
  10.3 0.6 all-gather.17.cloned.1.call-update
  10.9 0.1 all-gather.23.cloned.1.call-start
  11.0 0.6 all-gather.23.cloned.1.call-update
  11.6 5.5 multiply_reduce_fusion.4
  17.1 1.1 fusion.62
  18.2 39.5 %all-gather.13.cloned.1.call-done = bf16[1,1024,3072]{1,2,0:T(8,128)(2,1)} async-done(((bf16[1,1024,192]{1,2,0:T(8,128)(2,1)}), bf16[1,1024,3072]{1,2,0:T(8,128)(2,1)}) %all-gather.13.cloned.1.call-update) | async-done | bytes 6291472 | tf_op jit(solution)/shard_map/all_gather | solution.py:41
  57.6 8.6 %copy.28 = bf16[1,1024,3072]{2,1,0:T(8,128)(2,1)} copy(bf16[1,1024,3072]{1,2,0:T(8,128)(2,1)} %all-gather.13.cloned.1.call-done) | data formatting | bytes 12582912 | tf_op jit(solution)/shard_map/all_gather | solution.py:41
  66.2 42.3 %multiply_convert_fusion = (bf16[48,64,3072]{2,1,0:T(8,128)(2,1)}, f32[48,64,3072]{2,1,0:T(8,128)}) fusion(s32[]{:T(128)S(6)} %select_n.41, bf16[1024,3072]{1,0:T(8,128)(2,1)} %bitcast.155, f32[48,64,1024]{2,1,0:T(8,128)} %param.13, f32[48,64]{1,0:T(8,128)S(1)} %add_rsqrt_fusion.1), kind=kOutput, calls=%fused_computation.16 | convolution fusion | flops 19431161856 | bytes 75509760 | tf_op jit(solution)/shard_map/bsd,df->bsf/dot_general | solution.py:30
  108.6 52.5 %fusion.8 = bf16[48,64,3072]{2,1,0:T(8,128)(2,1)} fusion(f32[48,64,3072]{2,1,0:T(8,128)} %get-tuple-element.32, f32[48,64,1024]{2,1,0:T(8,128)} %param.16, s32[]{:T(128)S(6)} %select_n.41, bf16[3072,1024]{1,0:T(8,128)(2,1)} %bitcast.160), kind=kOutput, calls=%fused_computation.10 | convolution fusion | flops 19531825152 | bytes 75497472 | tf_op jit(solution)/shard_map/bsd,fd->bsf/dot_general | solution.py:30
  161.1 33.0 %multiply_reduce_fusion.2 = (f32[48,64]{1,0:T(8,128)S(1)}, f32[48,64,1024]{2,1,0:T(8,128)}) fusion(f32[48,64,1024]{2,1,0:T(8,128)} %param.13, f32[48,64]{1,0:T(8,128)S(1)} %add_rsqrt_fusion.1, bf16[48,64,3072]{2,1,0:T(8,128)(2,1)} %fusion.8, s32[]{:T(128)S(6)} %select_n.41, bf16[1024,3072]{1,0:T(8,128)(2,1)} %bitcast.156), kind=kOutput, calls=%fused_computation.36 | convolution fusion | flops 19349368832 | bytes 50356228 | tf_op jit(solution)/shard_map/bsf,df->bsd/dot_general | solution.py:30
  194.1 7.5 %fusion.66 = f32[1,192,1024]{2,1,0:T(8,128)} fusion(f32[48,64,1024]{2,1,0:T(8,128)} %param.16, bf16[48,64,3072]{2,1,0:T(8,128)(2,1)} %get-tuple-element.31), kind=kOutput, calls=%fused_computation.93 | convolution fusion | flops 1211105280 | bytes 14942208 | tf_op jit(solution)/shard_map/bsf,bsd->fd/dot_general | solution.py:30
  201.6 0.0 slice-done.3
  201.6 31.0 %multiply_reduce_fusion.3 = (f32[48,64]{1,0:T(8,128)S(1)}, f32[48,64,1024]{2,1,0:T(8,128)}) fusion(f32[48,64,1024]{2,1,0:T(8,128)} %param.14, bf16[48,64,3072]{2,1,0:T(8,128)(2,1)} %get-tuple-element.31, s32[]{:T(128)S(6)} %select_n.41, bf16[3072,1024]{1,0:T(8,128)(2,1)S(1)} %bitcast.163), kind=kOutput, calls=%fused_computation.41 | convolution fusion | flops 19349368832 | bytes 50343940 | tf_op jit(solution)/shard_map/bsf,fd->bsd/dot_general | solution.py:30
  232.6 0.6 copy-done.2
  233.2 7.9 %multiply_convert_fusion.2 = bf16[48,64,1024]{2,1,0:T(8,128)(2,1)} fusion(f32[48,64,1024]{2,1,0:T(8,128)} %get-tuple-element.34, f32[48,64]{1,0:T(8,128)S(1)} %add_rsqrt_fusion), kind=kLoop, calls=%fused_computation.44 | loop fusion | flops 6291456 | bytes 18886656 | tf_op jit(solution)/shard_map/convert_element_type | solution.py:64
  241.2 19.8 %convolution_convert_fusion.2 = bf16[48,64,16,128]{3,1,2,0:T(8,128)(2,1)} fusion(bf16[48,64,1024]{2,1,0:T(8,128)(2,1)} %multiply_convert_fusion.2, s32[]{:T(128)S(6)} %select_n.50, bf16[1024,16,128]{2,0,1:T(8,128)(2,1)} %bitcast.164), kind=kOutput, calls=%fused_computation.58 | convolution fusion | flops 12899581952 | bytes 23068676 | tf_op jit(solution)/shard_map/bsd,dhe->bshe/dot_general | solution.py:30
  261.0 19.6 %convolution_convert_fusion.1 = bf16[48,64,16,128]{3,1,2,0:T(8,128)(2,1)} fusion(bf16[48,64,1024]{2,1,0:T(8,128)(2,1)} %multiply_convert_fusion.2, s32[]{:T(128)S(6)} %select_n.50, bf16[1024,16,128]{2,0,1:T(8,128)(2,1)} %bitcast.166), kind=kOutput, calls=%fused_computation.57 | convolution fusion | flops 12899581952 | bytes 23068676 | tf_op jit(solution)/shard_map/bsd,dhe->bshe/dot_general | solution.py:30
  280.6 7.5 %fusion.63 = f32[1,1024,192]{1,2,0:T(8,128)} fusion(bf16[48,64,3072]{2,1,0:T(8,128)(2,1)} %fusion.8, f32[48,64,1024]{2,1,0:T(8,128)} %param.13, f32[48,64]{1,0:T(8,128)S(1)} %add_rsqrt_fusion.1), kind=kOutput, calls=%fused_computation.92 | convolution fusion | flops 1214251008 | bytes 14954496 | tf_op jit(solution)/shard_map/bsd,bsf->df/dot_general | solution.py:30
  288.1 17.7 %multiply_add_fusion.1 = f32[48,64,1024]{2,1,0:T(8,128)} fusion(f32[48,64,1024]{2,1,0:T(8,128)} %param.15, f32[48,64,1024]{2,1,0:T(8,128)} %get-tuple-element.38, f32[48,64,1024]{2,1,0:T(8,128)} %param.13, f32[48,64]{1,0:T(8,128)S(1)} %broadcast_multiply_fusion.1, f32[48,64]{1,0:T(8,128)S(1)} %add_rsqrt_fusion.1), kind=kLoop, calls=%fused_computation.35 | loop fusion | flops 15728640 | bytes 50356224 | tf_op jit(solution)/shard_map/add | solution.py:61
  305.8 19.6 %convolution_convert_fusion.3 = bf16[48,64,16,128]{3,1,2,0:T(8,128)(2,1)} fusion(bf16[48,64,1024]{2,1,0:T(8,128)(2,1)} %multiply_convert_fusion.2, s32[]{:T(128)S(6)} %select_n.50, bf16[1024,16,128]{2,0,1:T(8,128)(2,1)} %bitcast.168), kind=kOutput, calls=%fused_computation.59 | convolution fusion | flops 12899581952 | bytes 23068676 | tf_op jit(solution)/shard_map/bsd,dhe->bshe/dot_general | solution.py:30
  325.4 19.5 %convolution_convert_fusion = bf16[48,64,16,128]{3,1,2,0:T(8,128)(2,1)} fusion(f32[48,64,1024]{2,1,0:T(8,128)} %multiply_add_fusion.1, s32[]{:T(128)S(6)} %select_n.50, bf16[16,128,1024]{2,1,0:T(8,128)(2,1)} %bitcast.170), kind=kOutput, calls=%fused_computation.56 | convolution fusion | flops 12902727680 | bytes 29360132 | tf_op jit(solution)/shard_map/bid,hed->bihe/dot_general | solution.py:30
  344.9 15.4 %fusion.120 = f32[48,16,64,64]{2,3,1,0:T(8,128)} fusion(bf16[48,64,16,128]{3,1,2,0:T(8,128)(2,1)} %convolution_convert_fusion, bf16[48,64,16,128]{3,1,2,0:T(8,128)(2,1)S(1)} %copy-done), kind=kOutput, calls=%fused_computation.141 | convolution fusion | flops 805306368 | bytes 37748736 | tf_op jit(solution)/shard_map/bihe,bjhe->bhij/dot_general | solution.py:30
  360.3 0.0 copy-done.1
  360.3 22.3 %fusion.119 = (f32[48,16,64]{2,1,0:T(8,128)S(1)}, f32[48,16,64,64]{2,3,1,0:T(8,128)}) fusion(pred[48,64,64]{1,2,0:T(8,128)(4,1)S(1)} %copy-done.1, bf16[48,64,16,128]{3,1,2,0:T(8,128)(2,1)} %convolution_convert_fusion.2, bf16[48,64,16,128]{3,1,2,0:T(8,128)(2,1)} %convolution_convert_fusion.1), kind=kOutput, calls=%fused_computation.140 | convolution fusion | flops 817889344 | bytes 38141952 | tf_op jit(solution)/shard_map/sub | solution.py:70
  382.6 43.1 %convert_bitcast_fusion.2 = bf16[48,64,16,128]{3,1,2,0:T(8,128)(2,1)} fusion(bf16[48,64,16,128]{3,1,2,0:T(8,128)(2,1)} %convolution_convert_fusion.1, f32[48,16,64,64]{2,3,1,0:T(8,128)} %fusion.120, f32[48,16,64,64]{2,3,1,0:T(8,128)} %get-tuple-element.36, f32[48,16,64]{2,1,0:T(8,128)S(1)} %get-tuple-element.35), kind=kOutput, calls=%fused_computation.34 | convolution fusion | flops 833667136 | bytes 50528256 | tf_op jit(solution)/shard_map/bhij,bjhe->bihe/dot_general | solution.py:30
  425.7 40.6 %convert_bitcast_fusion.1 = bf16[48,64,16,128]{3,1,2,0:T(8,128)(2,1)} fusion(bf16[48,64,16,128]{3,1,2,0:T(8,128)(2,1)} %convolution_convert_fusion.2, f32[48,16,64,64]{2,3,1,0:T(8,128)} %fusion.120, f32[48,16,64,64]{2,3,1,0:T(8,128)} %get-tuple-element.36, f32[48,16,64]{2,1,0:T(8,128)S(1)} %get-tuple-element.35), kind=kOutput, calls=%fused_computation.33 | convolution fusion | flops 833667136 | bytes 50528256 | tf_op jit(solution)/shard_map/bhij,bihe->bjhe/dot_general | solution.py:30
  466.3 18.3 %convert_bitcast_fusion = bf16[48,64,16,128]{3,1,2,0:T(8,128)(2,1)} fusion(bf16[48,64,16,128]{3,1,2,0:T(8,128)(2,1)} %convolution_convert_fusion, f32[48,16,64,64]{2,3,1,0:T(8,128)} %get-tuple-element.36, f32[48,16,64]{2,1,0:T(8,128)S(1)} %get-tuple-element.35), kind=kOutput, calls=%fused_computation.32 | convolution fusion | flops 817889280 | bytes 37945344 | tf_op jit(solution)/shard_map/bhij,bihe->bjhe/dot_general | solution.py:30
  484.6 18.3 %convert_bitcast_fusion.3 = bf16[48,64,16,128]{3,1,2,0:T(8,128)(2,1)} fusion(bf16[48,64,16,128]{3,1,2,0:T(8,128)(2,1)} %convolution_convert_fusion.3, f32[48,16,64,64]{2,3,1,0:T(8,128)} %get-tuple-element.36, f32[48,16,64]{2,1,0:T(8,128)S(1)} %get-tuple-element.35), kind=kOutput, calls=%fused_computation.37 | convolution fusion | flops 817889280 | bytes 37945344 | tf_op jit(solution)/shard_map/bhij,bjhe->bihe/dot_general | solution.py:30
  503.0 6.8 %fusion.71 = f32[1,1,128,1024]{3,2,1,0:T(8,128)} fusion(f32[48,64,1024]{2,1,0:T(8,128)} %multiply_add_fusion.1, bf16[48,64,16,128]{3,1,2,0:T(8,128)(2,1)} %convert_bitcast_fusion.3), kind=kOutput, calls=%fused_computation.94 | convolution fusion | flops 808452096 | bytes 13893632 | tf_op jit(solution)/shard_map/bihe,bid->hed/dot_general | solution.py:30
  509.7 0.0 copy-done.7
  509.7 19.6 %bitcast_subtract_fusion = f32[48,64,1024]{2,1,0:T(8,128)} fusion(f32[48,64,1024]{2,1,0:T(8,128)} %param.13, bf16[48,64,16,128]{3,1,2,0:T(8,128)(2,1)} %convert_bitcast_fusion.3, s32[]{:T(128)S(6)} %select_n.50, bf16[16,128,1024]{2,1,0:T(8,128)(2,1)S(1)} %bitcast.171), kind=kOutput, calls=%fused_computation.29 | convolution fusion | flops 12890144768 | bytes 41943044 | tf_op jit(solution)/shard_map/bihe,hed->bid/dot_general | solution.py:30
  529.4 3.8 fusion.86
  533.2 18.2 %fusion.76 = f32[48,64,1024,1]{2,1,3,0:T(8,128)} fusion(bf16[48,64,16,128]{3,1,2,0:T(8,128)(2,1)} %convert_bitcast_fusion.2, s32[]{:T(128)S(6)} %select_n.50, bf16[1024,16,128]{2,0,1:T(8,128)(2,1)S(1)} %bitcast.165), kind=kOutput, calls=%fused_computation.95 | convolution fusion | flops 12886999040 | bytes 29360132 | tf_op jit(solution)/shard_map/bshe,dhe->bsd/dot_general | solution.py:30
  551.4 3.8 fusion.85
  555.2 0.0 copy-done.6
  555.2 18.3 %fusion.79 = f32[48,64,1024,1]{2,1,3,0:T(8,128)} fusion(bf16[48,64,16,128]{3,1,2,0:T(8,128)(2,1)} %convert_bitcast_fusion.1, s32[]{:T(128)S(6)} %select_n.50, bf16[1024,16,128]{2,0,1:T(8,128)(2,1)S(1)} %bitcast.167), kind=kOutput, calls=%fused_computation.96 | convolution fusion | flops 12886999040 | bytes 29360132 | tf_op jit(solution)/shard_map/bshe,dhe->bsd/dot_general | solution.py:30
  573.5 3.8 fusion.84
  577.3 27.4 %multiply_reduce_fusion.1 = (f32[48,64]{1,0:T(8,128)S(1)}, f32[48,64,1024]{2,1,0:T(8,128)}) fusion(f32[48,64,1024]{2,1,0:T(8,128)} %get-tuple-element.34, f32[48,64]{1,0:T(8,128)S(1)} %copy-done.3, bf16[48,64,16,128]{3,1,2,0:T(8,128)(2,1)} %convert_bitcast_fusion, s32[]{:T(128)S(6)} %select_n.50, bf16[1024,16,128]{2,0,1:T(8,128)(2,1)} %bitcast.169, ...), kind=kOutput, calls=%fused_computation.31 | convolution fusion | flops 12902724608 | bytes 67133440 | tf_op jit(solution)/shard_map/bshe,dhe->bsd/dot_general | solution.py:30
  604.7 17.7 %multiply_add_fusion = f32[48,64,1024]{2,1,0:T(8,128)} fusion(f32[48,64,1024]{2,1,0:T(8,128)} %param.16, f32[48,64,1024]{2,1,0:T(8,128)} %get-tuple-element.40, f32[48,64,1024]{2,1,0:T(8,128)} %get-tuple-element.34, f32[48,64]{1,0:T(8,128)S(1)} %broadcast_multiply_fusion, f32[48,64]{1,0:T(8,128)S(1)} %copy-done.3), kind=kLoop, calls=%fused_computation.30 | loop fusion | flops 15728640 | bytes 50356224 | tf_op jit(solution)/shard_map/add | solution.py:87
  (31 shorter events, 0.1 us)
Async XLA Ops:
  7.2 9.9 %copy-start.4 = (s32[48]{0:T(128)S(1)}, s32[48]{0:T(128)}, u32[]{:S(2)}) copy-start(s32[48]{0:T(128)} %param.17) | copy-start | bytes 580
  7.2 50.4 %all-gather.13.cloned.1.call-start = ((), (), s32[]{:S(2)}) async-start(), calls=%async_computation | async-start | bytes 6684672 | tf_op jit(solution)/shard_map/all_gather | solution.py:41
  8.0 100.6 %all-gather.15.cloned.1.call-start = ((), (), s32[]{:S(2)}) async-start(), calls=%async_computation.1 | async-start | bytes 6684672 | tf_op jit(solution)/shard_map/all_gather | solution.py:41
  8.8 232.4 %all-gather.19.cloned.1.call-start = ((), (), s32[]{:S(2)}) async-start(), calls=%async_computation.3 | async-start | bytes 4456448 | tf_op jit(solution)/shard_map/all_gather | solution.py:41
  9.6 251.4 %all-gather.21.cloned.1.call-start = ((), (), s32[]{:S(2)}) async-start(), calls=%async_computation.4 | async-start | bytes 4456448 | tf_op jit(solution)/shard_map/all_gather | solution.py:41
  10.2 295.6 %all-gather.17.cloned.1.call-start = ((), (), s32[]{:S(2)}) async-start(), calls=%async_computation.2 | async-start | bytes 4456448 | tf_op jit(solution)/shard_map/all_gather | solution.py:41
  10.9 314.5 %all-gather.23.cloned.1.call-start = ((), (), s32[]{:S(2)}) async-start(), calls=%async_computation.5 | async-start | bytes 4456448 | tf_op jit(solution)/shard_map/all_gather | solution.py:41
  194.1 7.5 %slice-start.2 = ((s8[6291456]{0:T(1024)(128)(4,1)}), s8[4194304]{0:T(1024)(128)(4,1)S(1)}, s32[]{:S(2)}) async-start(s8[6291456]{0:T(1024)(128)(4,1)} %bitcast.161), calls=%async_computation.8 | async-start | bytes 8388608
  194.1 7.5 %slice-start.3 = ((s8[6291456]{0:T(1024)(128)(4,1)}), s8[2097152]{0:T(1024)(128)(4,1)S(1)}, s32[]{:S(2)}) async-start(s8[6291456]{0:T(1024)(128)(4,1)} %bitcast.161), calls=%async_computation.9 | async-start | bytes 4194304
  232.6 0.6 copy-start.2
  325.4 19.5 %copy-start = (bf16[48,64,16,128]{3,1,2,0:T(8,128)(2,1)S(1)}, bf16[48,64,16,128]{3,1,2,0:T(8,128)(2,1)}, u32[]{:S(2)}) copy-start(bf16[48,64,16,128]{3,1,2,0:T(8,128)(2,1)} %convolution_convert_fusion.3) | copy-start | bytes 37748740
  344.9 15.4 %copy-start.1 = (pred[48,64,64]{1,2,0:T(8,128)(4,1)S(1)}, pred[48,64,64]{1,2,0:T(8,128)(4,1)}, u32[]{:S(2)}) copy-start(pred[48,64,64]{1,2,0:T(8,128)(4,1)} %fusion.62) | copy-start | bytes 589828
  503.0 6.8 %copy-start.7 = (bf16[16,1,128,1024]{3,2,1,0:T(8,128)(2,1)S(1)}, bf16[16,1,128,1024]{3,2,1,0:T(8,128)(2,1)}, u32[]{:S(2)}) copy-start(bf16[16,1,128,1024]{3,2,1,0:T(8,128)(2,1)} %all-gather.23.cloned.1.call-done) | copy-start | bytes 12582916
  503.0 26.4 %slice-start = ((s8[6291456]{0:T(1024)(128)(4,1)}), s8[4194304]{0:T(1024)(128)(4,1)S(1)}, s32[]{:S(2)}) async-start(s8[6291456]{0:T(1024)(128)(4,1)} %bitcast.153), calls=%async_computation.6 | async-start | bytes 8388608
  509.7 19.7 %slice-start.1 = ((s8[6291456]{0:T(1024)(128)(4,1)}), s8[2097152]{0:T(1024)(128)(4,1)S(1)}, s32[]{:S(2)}) async-start(s8[6291456]{0:T(1024)(128)(4,1)} %bitcast.153), calls=%async_computation.7 | async-start | bytes 4194304
  509.7 23.4 %copy-start.5 = (bf16[1,1024,16,128]{3,1,0,2:T(8,128)(2,1)S(1)}, bf16[1,1024,16,128]{3,1,0,2:T(8,128)(2,1)}, u32[]{:S(2)}) copy-start(bf16[1,1024,16,128]{3,1,0,2:T(8,128)(2,1)} %all-gather.19.cloned.1.call-done) | copy-start | bytes 12582916
  533.2 22.0 %copy-start.6 = (bf16[1,1024,16,128]{3,1,0,2:T(8,128)(2,1)S(1)}, bf16[1,1024,16,128]{3,1,0,2:T(8,128)(2,1)}, u32[]{:S(2)}) copy-start(bf16[1,1024,16,128]{3,1,0,2:T(8,128)(2,1)} %all-gather.21.cloned.1.call-done) | copy-start | bytes 12582916
  555.2 22.1 %copy-start.3 = (f32[48,64]{1,0:T(8,128)S(1)}, f32[48,64]{1,0:T(8,128)}, u32[]{:S(2)}) copy-start(f32[48,64]{1,0:T(8,128)} %copy-done.2) | copy-start | bytes 36868
Sparse Core Ops, SparseCore 0:
  9.7 47.9 all-gather.12
  59.3 41.5 all-gather.14
  102.4 37.2 all-gather.18
  141.2 36.8 all-gather.20
  179.6 36.8 all-gather.16
  218.0 36.8 all-gather.22

commit v2 on v1

--- a/solution.py
+++ b/solution.py
@@ -1,12 +1,303 @@
+import functools
+
 import jax
 import jax.numpy as jnp
 from jax import lax
+from jax.experimental import pallas as pl
+from jax.experimental.pallas import tpu as pltpu
 from jax.sharding import PartitionSpec as P
 
 F32 = jnp.float32
 BF16 = jnp.bfloat16
 EPS = 1e-5
 MASK_VALUE = -1e30
+CORES = 2
+GELU_A = 0.7978845608028654
+GELU_B = 0.044715
+
+
+def dot_nt(a, b):
+    return lax.dot_general(a, b, (((1,), (1,)), ((), ())), preferred_element_type=F32)
+
+
+def dot_nn(a, b):
+    return lax.dot_general(a, b, (((1,), (0,)), ((), ())), preferred_element_type=F32)
+
+
+def dot_tn(a, b):
+    return lax.dot_general(a, b, (((0,), (0,)), ((), ())), preferred_element_type=F32)
+
+
+def gelu_and_slope(x):
+    sq = x * x
+    t = jnp.tanh(GELU_A * (x + GELU_B * (sq * x)))
+    half = 0.5 * (1.0 + t)
+    slope = half + (0.5 * x) * (1.0 - t * t) * (GELU_A * (1.0 + (3.0 * GELU_B) * sq))
+    return x * half, slope
+
+
+def inv_rms_of(x):
+    return lax.rsqrt(jnp.mean(x * x, axis=-1, keepdims=True) + EPS)
+
+
+class Ring:
+    def __init__(self, n_tp):
+        self.chips = n_tp // CORES
+        me = lax.axis_index('tp')
+        self.core = lax.rem(me, CORES)
+        chip = lax.div(me, CORES)
+        up = lax.rem(chip + 1, self.chips) * CORES + self.core
+        down = lax.rem(chip + self.chips - 1, self.chips) * CORES + self.core
+        self.toward = (up, down)
+        self.sibling = chip * CORES + (1 - self.core)
+        self.far = self.chips // 2
+
+    def slot(self, hop, way):
+        return 2 * hop - 1 if hop == self.far else 2 * hop - 1 + way
+
+    def rows(self, slot, size):
+        return pl.ds(pl.multiple_of((slot * CORES + self.core) * size, 16), size)
+
+
+def remote(src, dst, send, recv, tp):
+    return pltpu.make_async_remote_copy(src_ref=src, dst_ref=dst, send_sem=send, recv_sem=recv,
+                                        device_id={'tp': tp}, device_id_type=pl.DeviceIdType.MESH)
+
+
+def entry_barrier(ring):
+    barrier = pltpu.get_barrier_semaphore()
+    for peer in (*ring.toward, ring.sibling):
+        pl.semaphore_signal(barrier, inc=1, device_id={'tp': peer}, device_id_type=pl.DeviceIdType.MESH)
+    pl.semaphore_wait(barrier, 3)
+
+
+def mlp_kernel(n_tp, tile, y1, y2, dy1, dy2, w1_own, w2_own, x2, dx1, dw1, dw2,
+               w1, w2, n1, e, acc_g, acc_d, part, from_sib, in_a, in_b, in_c, out_a, out_b,
+               own_sem, ring_send, ring_recv, d2d_send, d2d_recv, in_sem, out_sem, sib_send, sib_recv, dw_send, dw_recv,
+               dw_sem):
+    ring = Ring(n_tp)
+    far = ring.far
+    size = w1_own.shape[0]
+    rows_own = n1.shape[0]
+    base = ring.core * rows_own
+    own_w, all_w = (w1_own, w2_own), (w1, w2)
+    entry_barrier(ring)
+
+    def ring_copy(mat, way, hop):
+        src = own_w[mat] if hop == 1 else all_w[mat].at[ring.rows(ring.slot(hop - 1, way), size)]
+        return remote(src, all_w[mat].at[ring.rows(ring.slot(hop, way), size)],
+                      ring_send.at[mat, way, hop - 1], ring_recv.at[mat, way, hop - 1], ring.toward[way])
+
+    def has_hop(mat, way, hop):
+        return hop < far or (hop == far and mat == way)
+
+    def d2d_copy(mat, slot):
+        src = own_w[mat] if slot == 0 else all_w[mat].at[ring.rows(slot, size)]
+        return remote(src, all_w[mat].at[ring.rows(slot, size)], d2d_send.at[mat, slot], d2d_recv.at[mat, slot], ring.sibling)
+
+    def own_copy(mat):
+        return pltpu.make_async_copy(own_w[mat], all_w[mat].at[ring.rows(0, size)], own_sem.at[mat])
+
+    for mat in range(2):
+        for way in range(2):
+            ring_copy(mat, way, 1).start()
+    for mat in range(2):
+        own_copy(mat).start()
+        d2d_copy(mat, 0).start()
+
+    n_tiles = rows_own // tile
+
+    def hbm_tile(ref, t):
+        return ref.at[pl.ds(pl.multiple_of(base + t * tile, 16), tile)]
+
+    def fetch(src, dst, which, t, slot):
+        return pltpu.make_async_copy(hbm_tile(src, t), dst.at[slot], in_sem.at[which, slot])
+
+    def start_norm(t, slot):
+        fetch(y1, in_a, 0, t, slot).start()
+        fetch(dy2, in_b, 1, t, slot).start()
+
+    start_norm(0, 0)
+
+    def norm_body(t, _):
+        slot = lax.rem(t, 2)
+
+        @pl.when(t + 1 < n_tiles)
+        def _():
+            start_norm(t + 1, 1 - slot)
+
+        fetch(y1, in_a, 0, t, slot).wait()
+        fetch(dy2, in_b, 1, t, slot).wait()
+        here = pl.ds(pl.multiple_of(t * tile, 16), tile)
+        y = in_a[slot]
+        n1[here, :] = (y * inv_rms_of(y)).astype(BF16)
+        e[here, :] = in_b[slot].astype(BF16)
+        return 0
+
+    lax.fori_loop(0, n_tiles, norm_body, 0)
+
+    def products(here, first_row, width):
+        cols = pl.ds(first_row, width)
+        pre = dot_nt(n1[here, :], w1[cols, :])
+        d_act = dot_nt(e[here, :], w2[cols, :])
+        act, slope = gelu_and_slope(pre)
+        return act.astype(BF16), (d_act * slope).astype(BF16)
+
+    for mat in range(2):
+        own_copy(mat).wait()
+        d2d_copy(mat, 0).wait_recv()
+    big = 2 * tile
+    width = CORES * size
+    part[...] = jnp.zeros_like(part)
+
+    def own_body(t, _):
+        here = pl.ds(pl.multiple_of(t * big, 16), big)
+        act, d_pre = products(here, 0, width)
+        acc_g[here, :] = dot_nn(act, w2[0:width, :])
+        acc_d[here, :] = dot_nn(d_pre, w1[0:width, :])
+        part[0] += dot_tn(d_pre, n1[here, :])
+        part[1] += dot_tn(act, e[here, :])
+        return 0
+
+    lax.fori_loop(0, rows_own // big, own_body, 0)
+
+    def dw_copy(mat):
+        return remote(part.at[mat, pl.ds(pl.multiple_of((1 - ring.core) * size, 16), size)], from_sib.at[mat],
+                      dw_send.at[mat], dw_recv.at[mat], ring.sibling)
+
+    def pass_on(hop):
+        for mat in range(2):
+            for way in range(2):
+                if has_hop(mat, way, hop):
+                    ring_copy(mat, way, hop).wait_recv()
+                    if has_hop(mat, way, hop + 1):
+                        ring_copy(mat, way, hop + 1).start()
+                    d2d_copy(mat, ring.slot(hop, way)).start()
+        for mat in range(2):
+            for way in range(2):
+                if has_hop(mat, way, hop):
+                    d2d_copy(mat, ring.slot(hop, way)).wait_recv()
+
+    for hop in range(1, far):
+        pass_on(hop)
+        first_row = ring.slot(hop, 0) * width
+
+        def pair_body(t, _):
+            here = pl.ds(pl.multiple_of(t * big, 16), big)
+            act, d_pre = products(here, first_row, 2 * width)
+            cols = pl.ds(first_row, 2 * width)
+            acc_g[here, :] += dot_nn(act, w2[cols, :])
+            acc_d[here, :] += dot_nn(d_pre, w1[cols, :])
+            return 0
+
+        lax.fori_loop(0, rows_own // big, pair_body, 0)
+        if hop == 1:
+            for mat in range(2):
+                dw_copy(mat).start()
+
+    def start_last(t, slot):
+        for which, (src, dst) in enumerate(((y1, in_a), (y2, in_b), (dy1, in_c))):
+            fetch(src, dst, which, t, slot).start()
+
+    start_last(0, 0)
+    pass_on(far)
+    outs = ((out_a, x2), (out_b, dx1))
+
+    def out_copy(which, t, slot):
+        src, dst = outs[which]
+        return pltpu.make_async_copy(src.at[slot], hbm_tile(dst, t), out_sem.at[which, slot])
+
+    def sib_copy(which, t, slot):
+        src, dst = outs[which]
+        return remote(src.at[slot], hbm_tile(dst, t), sib_send.at[which, slot], sib_recv.at[which, t], ring.sibling)
+
+    far_row = ring.slot(far, 0) * width
+
+    def last_body(t, _):
+        slot = lax.rem(t, 2)
+        here = pl.ds(pl.multiple_of(t * tile, 16), tile)
+
+        @pl.when(t + 1 < n_tiles)
+        def _():
+            start_last(t + 1, 1 - slot)
+
+        @pl.when(t >= 2)
+        def _():
+            for which in range(2):
+                out_copy(which, t - 2, slot).wait()
+                sib_copy(which, t - 2, slot).wait_send()
+
+        act, d_pre = products(here, far_row, width)
+        cols = pl.ds(far_row, width)
+        total_g = acc_g[here, :] + dot_nn(act, w2[cols, :])
+        total_d = acc_d[here, :] + dot_nn(d_pre, w1[cols, :])
+        for which, (src, dst) in enumerate(((y1, in_a), (y2, in_b), (dy1, in_c))):
+            fetch(src, dst, which, t, slot).wait()
+        y = in_a[slot]
+        inv = inv_rms_of(y)
+        normed = y * inv
+        out_a[slot] = in_b[slot] - total_g
+        out_b[slot] = in_c[slot] + inv * (total_d - normed * jnp.mean(total_d * normed, axis=-1, keepdims=True))
+        for which in range(2):
+            out_copy(which, t, slot).start()
+            sib_copy(which, t, slot).start()
+        return 0
+
+    lax.fori_loop(0, n_tiles, last_body, 0)
+
+    for mat, dst in enumerate((dw1, dw2)):
+        dw_copy(mat).wait_recv()
+        mine = pl.ds(pl.multiple_of(ring.core * size, 16), size)
+        from_sib[mat] = from_sib[mat] + part[mat, mine, :]
+        pltpu.make_async_copy(from_sib.at[mat], dst, dw_sem.at[mat]).start()
+
+    for mat, dst in enumerate((dw1, dw2)):
+        pltpu.make_async_copy(from_sib.at[mat], dst, dw_sem.at[mat]).wait()
+        dw_copy(mat).wait_send()
+        for way in range(2):
+            for hop in range(1, far + 1):
+                if has_hop(mat, way, hop):
+                    ring_copy(mat, way, hop).wait_send()
+        for slot in range(ring.chips):
+            d2d_copy(mat, slot).wait_send()
+    for t in range(max(n_tiles - 2, 0), n_tiles):
+        for which in range(2):
+            out_copy(which, t, t % 2).wait()
+            sib_copy(which, t, t % 2).wait_send()
+    for t in range(n_tiles):
+        for which in range(2):
+            sib_copy(which, t, t % 2).wait_recv()
+
+
+def mlp_back(n_tp, y1, y2, dy1, dy2, w1_own, w2_own, tile=256):
+    tokens, d = y1.shape
+    size = w1_own.shape[0]
+    chips = n_tp // CORES
+    half = tokens // CORES
+    n_tiles = half // tile
+    hidden = n_tp * size
+    hbm = pl.BlockSpec(memory_space=pl.ANY)
+    dma = pltpu.SemaphoreType.DMA
+    flops = 8 * half * d * hidden
+    return pl.pallas_call(
+        functools.partial(mlp_kernel, n_tp, tile),
+        name='mlp_back',
+        out_shape=[jax.ShapeDtypeStruct((tokens, d), F32)] * 2 + [jax.ShapeDtypeStruct((size, d), F32)] * 2,
+        in_specs=[hbm] * 6,
+        out_specs=[hbm] * 4,
+        scratch_shapes=[
+            pltpu.VMEM((hidden, d), BF16), pltpu.VMEM((hidden, d), BF16),
+            pltpu.VMEM((half, d), BF16), pltpu.VMEM((half, d), BF16),
+            pltpu.VMEM((half, d), F32), pltpu.VMEM((half, d), F32),
+            pltpu.VMEM((2, CORES * size, d), F32), pltpu.VMEM((2, size, d), F32),
+            pltpu.VMEM((2, tile, d), F32), pltpu.VMEM((2, tile, d), F32), pltpu.VMEM((2, tile, d), F32),
+            pltpu.VMEM((2, tile, d), F32), pltpu.VMEM((2, tile, d), F32),
+            dma((2,)), dma((2, 2, chips // 2)), dma((2, 2, chips // 2)), dma((2, chips)), dma((2, chips)),
+            dma((3, 2)), dma((2, 2)), dma((2, 2)), dma((2, n_tiles)), dma((2,)), dma((2,)), dma((2,)),
+        ],
+        compiler_params=pltpu.CompilerParams(collective_id=0, has_side_effects=True, vmem_limit_bytes=60 * 2 ** 20),
+        cost_estimate=pl.CostEstimate(flops=flops, bytes_accessed=8 * tokens * d * 4, transcendentals=half * hidden),
+    )(y1, y2, dy1, dy2, w1_own, w2_own)
 
 
 def rms_norm(x_val):
@@ -30,7 +321,7 @@
     return jnp.einsum(spec, a, b, preferred_element_type=F32)
 
 
-def block_back(carry, seq_lens, layer_w, tp_idx):
+def block_back(carry, seq_lens, layer_w, tp_idx, n_tp):
     y_one, y_two, dy_one, dy_two = carry
     own_q, own_k, own_v, own_o, own_up, own_down = layer_w
     seq_len = y_one.shape[1]
@@ -42,23 +333,11 @@
         size = w.shape[axis]
         return jnp.roll(full, -tp_idx * size, axis=axis)
 
-    w_up, w_down = gathered(own_up, 1), gathered(own_down, 0)
     w_query, w_key, w_value, w_out = gathered(own_q, 1), gathered(own_k, 1), gathered(own_v, 1), gathered(own_o, 0)
-    own_ff = own_up.shape[1]
-
-    norm_g, inv_g = rms_norm(y_one)
-    norm_g_b = norm_g.astype(BF16)
-    pre_act = dot('bsd,df->bsf', norm_g_b, w_up)
-    act_val, gelu_back = jax.vjp(jax.nn.gelu, pre_act)
-    act_b = act_val.astype(BF16)
-    x_two = y_two - dot('bsf,fd->bsd', act_b, w_down)
-    dy2_b = dy_two.astype(BF16)
-    d_act = dot('bsd,fd->bsf', dy2_b, w_down)
-    d_pre = gelu_back(d_act)[0].astype(BF16)
-    dw_down = dot('bsf,bsd->fd', act_b[..., :own_ff], dy2_b)
-    dw_up = dot('bsd,bsf->df', norm_g_b, d_pre[..., :own_ff])
-    grad_norm_g = dot('bsf,df->bsd', d_pre, w_up)
-    dy_one = dy_one + rms_back(norm_g, inv_g, grad_norm_g)
+    flat = (-1, y_one.shape[-1])
+    x_two, dy_one, dw_up, dw_down = mlp_back(n_tp, y_one.reshape(flat), y_two.reshape(flat), dy_one.reshape(flat),
+                                             dy_two.reshape(flat), own_up.T, own_down)
+    x_two, dy_one, dw_up = x_two.reshape(y_one.shape), dy_one.reshape(y_one.shape), dw_up.T
 
     norm_f, inv_f = rms_norm(x_two)
     norm_f_b = norm_f.astype(BF16)
@@ -107,7 +386,7 @@
         grads_by_layer = [None] * n_layers
         for layer_idx in reversed(range(n_layers)):
             layer_w = tuple(w_stack[layer_idx] for w_stack in weights)
-            carry, grads_by_layer[layer_idx] = block_back(carry, seq_lens, layer_w, tp_idx)
+            carry, grads_by_layer[layer_idx] = block_back(carry, seq_lens, layer_w, tp_idx, mesh.shape['tp'])
         return carry + stack_grads(grads_by_layer)
 
     return jax.shard_map(local_fn, mesh=mesh,

time: 638 us -> 576 us (0.903)
  matrix products: 512 us -> 347 us
  Pallas kernels: 0 us -> 133 us
  waiting for transfers between devices: 43.3 us -> 2.75 us
  local copies, waits for them, and re-layouts: 9.24 us -> 26.2 us
    dot_general x23 -> x17, matrix products: 490 us -> 325 us  [dot(): return jnp.einsum(spec, a, b, preferred_element_type=F32)]
    pallas_call x0 -> x1, Pallas kernels: none -> 133 us  [mlp_back(): pl.pallas_call(functools.partial(mlp_kernel, n_tp, tile), name='mlp_back'...]
    all_gather x6 -> x4, waiting for transfers between devices: 39.5 us -> 0.03 us  [gathered(): full = lax.all_gather(w, 'tp', axis=axis, tiled=True)]
    unnamed x24 -> x22, local copies, waits for them, and re-layouts: 0.63 us -> 26.1 us
    add x1 -> x0, other arithmetic: 17.7 us -> none  [block_back(): dy_one = dy_one + rms_back(norm_g, inv_g, grad_norm_g)]
    all_gather x1 -> x0, local copies, waits for them, and re-layouts: 8.61 us -> none  [gathered(): full = lax.all_gather(w, 'tp', axis=axis, tiled=True)]
    convert_element_type x0 -> x1, other arithmetic: none -> 8.2 us  [block_back(): dy1_b = dy_one.astype(BF16)]
    convert_element_type x1 -> x2, other arithmetic: 7.95 us -> 16 us  [block_back(): norm_f_b = norm_f.astype(BF16)]
  transfers between devices with their start and end apart: 6 -> 4, of which waited for: 1 -> 0; matrix products, arithmetic and copies ran while one was open for 43% -> 16% of each run, Pallas kernels for 0% -> 23%
where the time goes in v2:
time: 576 us; the launch traced here: 568 us
  matrix products  347 us (60%)
  Pallas kernels  133 us (23%)
  other arithmetic  44.4 us (8%)
  local copies, waits for them, and re-layouts  26.2 us (5%)
  between operations  14.1 us (2%)
    dot_general x17, matrix products, dot(): return jnp.einsum(spec, a, b, preferred_element_type=F32)  325 us
    pallas_call x1, Pallas kernels, mlp_back(): pl.pallas_call(functools.partial(mlp_kernel, n_tp, tile), name='mlp_back'...  133 us
    unnamed x22, local copies, waits for them, and re-layouts  26.1 us
    sub x1, matrix products, block_back(): probs = jax.nn.softmax(scores, axis=-1)  21.9 us
    convert_element_type x2, other arithmetic, block_back(): norm_f_b = norm_f.astype(BF16)  16 us
    add x1, other arithmetic, block_back(): dx_two = dy_two + rms_back(norm_f, inv_f, grad_norm_f)  14.4 us
  transfers between devices with their start and end apart: 4, of which 0 were waited for; matrix products, arithmetic and copies ran while one was open for 16% of the time, Pallas kernels for 23%

profile of v2, /device:TPU:21, one launch (start us, length us, event | category | flops | bytes accessed | tf_op | source)
XLA Modules:
  0.0 567.9 jit_solution(14533539537492212761)
XLA Ops:
  7.2 0.1 all-gather.9.cloned.1.call-start
  7.3 0.7 all-gather.9.cloned.1.call-update
  8.0 0.1 all-gather.13.cloned.1.call-start
  8.1 0.7 all-gather.13.cloned.1.call-update
  8.8 0.1 all-gather.15.cloned.1.call-start
  8.9 0.7 all-gather.15.cloned.1.call-update
  9.6 0.1 all-gather.11.cloned.1.call-start
  9.7 0.6 all-gather.11.cloned.1.call-update
  10.3 133.4 %mlp_back.1 = (f32[3072,1024]{1,0:T(8,128)}, f32[3072,1024]{1,0:T(8,128)}, f32[192,1024]{1,0:T(8,128)}, f32[192,1024]{1,0:T(8,128)}) custom-call(f32[3072,1024]{1,0:T(8,128)} %bitcast.146, f32[3072,1024]{1,0:T(8,128)} %bitcast.144, f32[3072,1024]{1,0:T(8,128)} %bitcast.145, f32[3072,1024]{1,0:T(8,128)} %bitcast.133, bf16[192,1024]{1,0:T(8,128)(2,1)} %bitcast.155, ...), custom_call_target="tpu_custom_call" | custom-call | flops 38654705664 | bytes 100663296 | tf_op jit(solution)/shard_map/mlp_back/pallas_call | solution.py:282
  143.7 5.5 multiply_reduce_fusion.2
  149.2 0.1 rsqrt.13
  149.2 7.9 %multiply_convert_fusion.1 = bf16[3072,1024]{1,0:T(8,128)(2,1)} fusion(f32[3072,1024]{1,0:T(8,128)} %get-tuple-element.15, f32[3072]{0:T(1024)S(1)} %add_rsqrt_fusion), kind=kLoop, calls=%fused_computation.11 | loop fusion | flops 6291456 | bytes 18886656 | tf_op jit(solution)/shard_map/convert_element_type | solution.py:343
  157.1 8.1 %fusion.19 = bf16[48,64,1024,1]{2,1,3,0:T(8,128)(2,1)} fusion(f32[48,64,1024]{2,1,0:T(8,128)} %bitcast.126, f32[48,64]{1,0:T(8,128)S(1)} %rsqrt.13), kind=kLoop, calls=%fused_computation.38 | loop fusion | flops 6291456 | bytes 18886656 | tf_op jit(solution)/shard_map/convert_element_type | solution.py:343
  165.2 0.0 copy-done.3
  165.2 8.2 %convert_element_type.78 = bf16[3072,1024]{1,0:T(8,128)(2,1)} convert(f32[3072,1024]{1,0:T(8,128)} %get-tuple-element.16) | non-fusion elementwise | flops 3145728 | bytes 18874368 | tf_op jit(solution)/shard_map/convert_element_type | solution.py:353
  173.4 0.0 copy-done.5
  173.4 0.3 fusion.32
  173.7 0.0 all-gather.9.cloned.1.call-done
  173.8 19.6 %convolution_convert_fusion.3 = bf16[48,64,16,128]{3,1,2,0:T(8,128)(2,1)} fusion(bf16[48,64,1024,1]{2,1,3,0:T(8,128)(2,1)} %fusion.19, s32[]{:T(128)S(6)} %select_n.32, bf16[1024,16,128]{2,0,1:T(8,128)(2,1)} %bitcast.147), kind=kOutput, calls=%fused_computation.37 | convolution fusion | flops 12899581952 | bytes 23068676 | tf_op jit(solution)/shard_map/bsd,dhe->bshe/dot_general | solution.py:321
  193.4 20.0 %convolution_convert_fusion.1 = bf16[48,64,16,128]{3,1,2,0:T(8,128)(2,1)} fusion(bf16[48,64,1024,1]{2,1,3,0:T(8,128)(2,1)} %fusion.19, s32[]{:T(128)S(6)} %select_n.32, bf16[1024,16,128]{2,0,1:T(8,128)(2,1)} %bitcast.151), kind=kOutput, calls=%fused_computation.35 | convolution fusion | flops 12899581952 | bytes 23068676 | tf_op jit(solution)/shard_map/bsd,dhe->bshe/dot_general | solution.py:321
  213.4 18.8 %convolution_convert_fusion = bf16[48,64,16,128]{3,1,2,0:T(8,128)(2,1)} fusion(f32[48,64,1024]{2,1,0:T(8,128)} %bitcast.130, s32[]{:T(128)S(6)} %select_n.32, bf16[16,128,1024]{2,1,0:T(8,128)(2,1)} %bitcast.149), kind=kOutput, calls=%fused_computation.34 | convolution fusion | flops 12902727680 | bytes 29360132 | tf_op jit(solution)/shard_map/bid,hed->bihe/dot_general | solution.py:321
  232.2 19.6 %convolution_convert_fusion.2 = bf16[48,64,16,128]{3,1,2,0:T(8,128)(2,1)} fusion(bf16[48,64,1024,1]{2,1,3,0:T(8,128)(2,1)} %fusion.19, s32[]{:T(128)S(6)} %select_n.32, bf16[1024,16,128]{2,0,1:T(8,128)(2,1)} %bitcast.153), kind=kOutput, calls=%fused_computation.36 | convolution fusion | flops 12899581952 | bytes 23068676 | tf_op jit(solution)/shard_map/bsd,dhe->bshe/dot_general | solution.py:321
  251.7 20.4 %fusion.71 = f32[48,16,64,64]{2,3,1,0:T(8,128)} fusion(bf16[48,64,16,128]{3,1,2,0:T(8,128)(2,1)} %convolution_convert_fusion, bf16[48,64,16,128]{3,1,2,0:T(8,128)(2,1)} %convolution_convert_fusion.3), kind=kOutput, calls=%fused_computation.90 | convolution fusion | flops 805306368 | bytes 37748736 | tf_op jit(solution)/shard_map/bihe,bjhe->bhij/dot_general | solution.py:321
  272.2 21.9 %fusion.70 = (f32[48,16,64]{2,1,0:T(8,128)S(1)}, f32[48,16,64,64]{2,3,1,0:T(8,128)}) fusion(pred[48,64,64]{1,2,0:T(8,128)(4,1)S(1)} %fusion.32, bf16[48,64,16,128]{3,1,2,0:T(8,128)(2,1)} %convolution_convert_fusion.2, bf16[48,64,16,128]{3,1,2,0:T(8,128)(2,1)} %convolution_convert_fusion.1), kind=kOutput, calls=%fused_computation.89 | convolution fusion | flops 817889344 | bytes 38141952 | tf_op jit(solution)/shard_map/sub | solution.py:349
  294.1 43.7 %convert_bitcast_fusion.2 = bf16[48,64,16,128]{3,1,2,0:T(8,128)(2,1)} fusion(bf16[48,64,16,128]{3,1,2,0:T(8,128)(2,1)} %convolution_convert_fusion.1, f32[48,16,64,64]{2,3,1,0:T(8,128)} %fusion.71, f32[48,16,64,64]{2,3,1,0:T(8,128)} %get-tuple-element.40, f32[48,16,64]{2,1,0:T(8,128)S(1)} %get-tuple-element.39), kind=kOutput, calls=%fused_computation.16 | convolution fusion | flops 833667136 | bytes 50528256 | tf_op jit(solution)/shard_map/bhij,bjhe->bihe/dot_general | solution.py:321
  337.8 40.9 %convert_bitcast_fusion.1 = bf16[48,64,16,128]{3,1,2,0:T(8,128)(2,1)} fusion(bf16[48,64,16,128]{3,1,2,0:T(8,128)(2,1)} %convolution_convert_fusion.2, f32[48,16,64,64]{2,3,1,0:T(8,128)} %fusion.71, f32[48,16,64,64]{2,3,1,0:T(8,128)} %get-tuple-element.40, f32[48,16,64]{2,1,0:T(8,128)S(1)} %get-tuple-element.39), kind=kOutput, calls=%fused_computation.15 | convolution fusion | flops 833667136 | bytes 50528256 | tf_op jit(solution)/shard_map/bhij,bihe->bjhe/dot_general | solution.py:321
  378.7 18.4 %convert_bitcast_fusion = bf16[48,64,16,128]{3,1,2,0:T(8,128)(2,1)} fusion(bf16[48,64,16,128]{3,1,2,0:T(8,128)(2,1)} %convolution_convert_fusion, f32[48,16,64,64]{2,3,1,0:T(8,128)} %get-tuple-element.40, f32[48,16,64]{2,1,0:T(8,128)S(1)} %get-tuple-element.39), kind=kOutput, calls=%fused_computation.14 | convolution fusion | flops 817889280 | bytes 37945344 | tf_op jit(solution)/shard_map/bhij,bihe->bjhe/dot_general | solution.py:321
  397.1 19.3 %fusion.35 = f32[48,64,1024,1]{2,1,3,0:T(8,128)} fusion(bf16[48,64,16,128]{3,1,2,0:T(8,128)(2,1)} %convert_bitcast_fusion.2, s32[]{:T(128)S(6)} %select_n.32, bf16[1024,16,128]{2,0,1:T(8,128)(2,1)} %bitcast.154), kind=kOutput, calls=%fused_computation.54 | convolution fusion | flops 12886999040 | bytes 29360132 | tf_op jit(solution)/shard_map/bshe,dhe->bsd/dot_general | solution.py:321
  416.4 0.0 slice-done
  416.4 0.0 slice-done.1
  416.5 3.8 fusion.45
  420.2 0.0 copy-done.6
  420.2 18.5 %fusion.38 = f32[48,64,1024,1]{2,1,3,0:T(8,128)} fusion(bf16[48,64,16,128]{3,1,2,0:T(8,128)(2,1)} %convert_bitcast_fusion.1, s32[]{:T(128)S(6)} %select_n.32, bf16[1024,16,128]{2,0,1:T(8,128)(2,1)S(1)} %bitcast.152), kind=kOutput, calls=%fused_computation.55 | convolution fusion | flops 12886999040 | bytes 29360132 | tf_op jit(solution)/shard_map/bshe,dhe->bsd/dot_general | solution.py:321
  438.7 3.7 fusion.44
  442.5 18.4 %convert_bitcast_fusion.3 = bf16[48,64,16,128]{3,1,2,0:T(8,128)(2,1)} fusion(bf16[48,64,16,128]{3,1,2,0:T(8,128)(2,1)} %convolution_convert_fusion.3, f32[48,16,64,64]{2,3,1,0:T(8,128)} %get-tuple-element.40, f32[48,16,64]{2,1,0:T(8,128)S(1)} %get-tuple-element.39), kind=kOutput, calls=%fused_computation.17 | convolution fusion | flops 817889280 | bytes 37945344 | tf_op jit(solution)/shard_map/bhij,bjhe->bihe/dot_general | solution.py:321
  460.9 5.6 fusion.43
  466.5 0.0 copy-done.4
  466.5 27.6 %multiply_reduce_fusion.1 = (f32[48,64]{1,0:T(8,128)S(1)}, f32[48,64,1024]{2,1,0:T(8,128)}) fusion(f32[48,64,1024]{2,1,0:T(8,128)} %bitcast.127, f32[48,64]{1,0:T(8,128)S(1)} %copy-done.4, bf16[48,64,16,128]{3,1,2,0:T(8,128)(2,1)} %convert_bitcast_fusion, s32[]{:T(128)S(6)} %select_n.32, bf16[1024,16,128]{2,0,1:T(8,128)(2,1)} %bitcast.148, ...), kind=kOutput, calls=%fused_computation.13 | convolution fusion | flops 12902724608 | bytes 67133440 | tf_op jit(solution)/shard_map/bshe,dhe->bsd/dot_general | solution.py:321
  494.1 0.0 copy-start
  494.1 21.7 %bitcast_subtract_fusion = f32[48,64,1024]{2,1,0:T(8,128)} fusion(f32[48,64,1024]{2,1,0:T(8,128)} %param.13, bf16[48,64,16,128]{3,1,2,0:T(8,128)(2,1)} %convert_bitcast_fusion.3, s32[]{:T(128)S(6)} %select_n.32, bf16[16,128,1024]{2,1,0:T(8,128)(2,1)} %bitcast.150), kind=kOutput, calls=%fused_computation.10 | convolution fusion | flops 12890144768 | bytes 41943044 | tf_op jit(solution)/shard_map/bihe,hed->bid/dot_general | solution.py:321
  515.8 4.9 convolution_bitcast_fusion
  520.6 0.0 copy-done
  520.6 14.4 %multiply_add_fusion = f32[48,64,1024]{2,1,0:T(8,128)} fusion(f32[48,64,1024]{2,1,0:T(8,128)} %param.16, f32[48,64,1024]{2,1,0:T(8,128)S(1)} %copy-done, f32[48,64,1024]{2,1,0:T(8,128)} %bitcast.128, f32[48,64]{1,0:T(8,128)S(1)} %broadcast_multiply_fusion, f32[48,64]{1,0:T(8,128)S(1)} %copy-done.4), kind=kLoop, calls=%fused_computation.12 | loop fusion | flops 15728640 | bytes 50356224 | tf_op jit(solution)/shard_map/add | solution.py:366
  535.0 12.1 %copy.47 = f32[48,64,1024]{2,1,0:T(8,128)} copy(f32[48,64,1024]{2,1,0:T(8,128)} %bitcast.129) | data formatting | bytes 25165824
  547.1 12.2 %copy.48 = f32[48,64,1024]{2,1,0:T(8,128)} copy(f32[48,64,1024]{2,1,0:T(8,128)} %bitcast.131) | data formatting | bytes 25165824
  559.4 0.0 copy-done.2
  559.4 0.9 copy.49
  560.2 0.9 copy.50
  (16 shorter events, 0.0 us)
Async XLA Ops:
  7.2 166.6 %all-gather.9.cloned.1.call-start = ((), (), s32[]{:S(2)}) async-start(), calls=%async_computation | async-start | bytes 4456448 | tf_op jit(solution)/shard_map/all_gather | solution.py:332
  8.0 185.4 %all-gather.13.cloned.1.call-start = ((), (), s32[]{:S(2)}) async-start(), calls=%async_computation.2 | async-start | bytes 4456448 | tf_op jit(solution)/shard_map/all_gather | solution.py:332
  8.8 204.6 %all-gather.15.cloned.1.call-start = ((), (), s32[]{:S(2)}) async-start(), calls=%async_computation.3 | async-start | bytes 4456448 | tf_op jit(solution)/shard_map/all_gather | solution.py:332
  9.6 222.6 %all-gather.11.cloned.1.call-start = ((), (), s32[]{:S(2)}) async-start(), calls=%async_computation.1 | async-start | bytes 4456448 | tf_op jit(solution)/shard_map/all_gather | solution.py:332
  149.2 16.0 %copy-start.3 = (f32[48,64]{1,0:T(8,128)}, f32[48,64]{1,0:T(8,128)S(1)}, u32[]{:S(2)}) copy-start(f32[48,64]{1,0:T(8,128)S(1)} %rsqrt.13) | copy-start | bytes 36868
  165.2 8.2 %copy-start.5 = (s32[48]{0:T(128)S(1)}, s32[48]{0:T(128)}, u32[]{:S(2)}) copy-start(s32[48]{0:T(128)} %param.17) | copy-start | bytes 580
  337.8 78.7 %slice-start = ((s8[6291456]{0:T(1024)(128)(4,1)}), s8[2097152]{0:T(1024)(128)(4,1)S(1)}, s32[]{:S(2)}) async-start(s8[6291456]{0:T(1024)(128)(4,1)} %bitcast.135), calls=%async_computation.4 | async-start | bytes 4194304
  378.7 37.8 %slice-start.1 = ((s8[6291456]{0:T(1024)(128)(4,1)}), s8[4194304]{0:T(1024)(128)(4,1)S(1)}, s32[]{:S(2)}) async-start(s8[6291456]{0:T(1024)(128)(4,1)} %bitcast.135), calls=%async_computation.5 | async-start | bytes 8388608
  397.1 23.1 %copy-start.6 = (bf16[1,1024,16,128]{3,1,0,2:T(8,128)(2,1)S(1)}, bf16[1,1024,16,128]{3,1,0,2:T(8,128)(2,1)}, u32[]{:S(2)}) copy-start(bf16[1,1024,16,128]{3,1,0,2:T(8,128)(2,1)} %all-gather.13.cloned.1.call-done) | copy-start | bytes 12582916
  442.5 24.0 %copy-start.4 = (f32[48,64]{1,0:T(8,128)S(1)}, f32[48,64]{1,0:T(8,128)}, u32[]{:S(2)}) copy-start(f32[48,64]{1,0:T(8,128)} %copy-done.3) | copy-start | bytes 36868
  494.1 26.5 %copy-start = (f32[48,64,1024]{2,1,0:T(8,128)S(1)}, f32[48,64,1024]{2,1,0:T(8,128)}, u32[]{:S(2)}) copy-start(f32[48,64,1024]{2,1,0:T(8,128)} %get-tuple-element.42) | copy-start | bytes 37748740
  547.1 12.2 %copy-start.2 = (f32[192,1024]{1,0:T(8,128)S(1)}, f32[192,1024]{1,0:T(8,128)}, u32[]{:S(2)}) copy-start(f32[192,1024]{1,0:T(8,128)} %get-tuple-element.17) | copy-start | bytes 2359300
  547.1 13.1 %copy-start.1 = (f32[192,1024]{1,0:T(8,128)S(1)}, f32[192,1024]{1,0:T(8,128)}, u32[]{:S(2)}) copy-start(f32[192,1024]{1,0:T(8,128)} %get-tuple-element.18) | copy-start | bytes 2359300
Sparse Core Ops, SparseCore 0:
  9.6 57.8 all-gather.8
  69.2 50.5 all-gather.12
  121.5 37.2 all-gather.14
  160.2 36.8 all-gather.10
